TPU v7x, 256 devices: a whole 4x4x8 slice. The times are simulated.
256 devices in a mesh: row: 16 (over y, x), col: 16 (over z, core).
Axes of the slice: x: 4, y: 4, z: 8, core: 2. Of those that a mesh axis runs over, the one named last changes fastest.
Arguments:
- trail: float32 [2, 16, 512, 2, 16, 512], P(None, 'row', None, None, 'col'), may hold values from -6 to 6
- panel: float32 [2, 16, 512, 512], P(None, 'row', None, 'col'), may hold values from -6 to 6
- row_basis: float32 [2, 16, 64, 512], P(None, 'row', None, 'col'), may hold values from -0.75 to 0.75
- row_coeff: float32 [2, 16, 64, 512], P(None, 'row', None, 'col'), may hold values from -0.25 to 0.25
- col_basis: float32 [2, 16, 64, 512], P(None, 'col', None, 'row'), may hold values from -0.75 to 0.75
- col_scaled: float32 [2, 16, 64, 512], P(None, 'col', None, 'row'), may hold values from -0.25 to 0.25
- pivot_basis: float32 [64, 512], P(None, 'col'), may hold values from -0.75 to 0.75
- pivot_scaled: float32 [64, 512], replicated, may hold values from -0.25 to 0.25
- sketch: float32 [64, 512], replicated, may hold values from -6 to 6
- perm: int32 [512], replicated, may hold values from 0 to 511, each once
- pair_kind: int32 [256], replicated, may hold values from 0 to 1
- pivot_values: float32 [3, 256], replicated, may hold values from -3 to 3, as said below
Outputs:
- trail_out: float32 [2, 16, 512, 2, 16, 512], P(None, 'row', None, None, 'col')
- basis_out: float32 [2, 16, 64, 512], P(None, 'row')
- coeff_out: float32 [2, 16, 64, 512], P(None, 'row')
Inputs may be any that keep to these rules, and one draw needn't show every extreme that they name: `pivot_values`: rows 0 and 1 have magnitudes between 0.5 and 0.7; row 2 has magnitude 1.2 or more.
All inputs are finite; a program needn't handle non-finite values.
Results may differ from a plain program's by a relative error of at most 0.00013.
Values sent between devices are 32-bit elements; how exact they have to be, the bound alone decides.
A program may use at most 64 MiB of HBM per device.

v0:
```python
import jax
import jax.numpy as jnp
from jax import lax
from jax.sharding import PartitionSpec as P


def gather_turned(arrays, axis, dims):
    turned = [jnp.moveaxis(a, dim, 0) for a, dim in zip(arrays, dims)]
    both = jnp.concatenate([t.reshape(len(t), -1) for t in turned], axis=1)
    filled, at, outs = (lax.all_gather(both, axis, axis=0, tiled=True), 0, [])
    for t, dim in zip(turned, dims):
        share = filled[:, at : at + t[0].size].reshape(-1, *t.shape[1:])
        outs.append(jnp.moveaxis(share, 0, dim))
        at += t[0].size
    return tuple(outs)


def total_of_pieces(array, axis):
    return lax.all_gather(array, axis).sum(0)


def pair_apply(rows, pair_kind, pivot_values):
    shaped = rows.reshape(rows.shape[:-1] + (rows.shape[-1] // 2, 2))
    first_in = shaped[..., 0]
    second_in = shaped[..., 1]
    diag_one = pivot_values[0]
    diag_two = pivot_values[1]
    offdiag = pivot_values[2]
    determinant = diag_one * diag_two - offdiag * offdiag
    twin = pair_kind == 1
    first = jnp.where(
        twin, (first_in * diag_two - second_in * offdiag) / determinant, first_in / diag_one
    )
    second = jnp.where(
        twin, (second_in * diag_one - first_in * offdiag) / determinant, second_in / diag_two
    )
    return jnp.stack([first, second], axis=-1).reshape(rows.shape)


def tri_solve(lower, rhs):
    return jax.vmap(lambda low, right: jax.scipy.linalg.solve_triangular(low, right, lower=True))(
        lower, rhs
    )


def body(
    trail,
    panel,
    row_basis,
    row_coeff,
    col_basis,
    col_scaled,
    pivot_basis,
    pivot_scaled,
    sketch,
    perm,
    pair_kind,
    pivot_values,
):
    highest = lax.Precision.HIGHEST
    width = sketch.shape[1]
    block = panel.shape[3]
    xrows, yrows = gather_turned((row_basis, row_coeff), "col", (3, 3))
    zcols, gcols = gather_turned((col_basis, col_scaled), "row", (3, 3))
    xrows = xrows[:, 0]
    yrows = yrows[:, 0]
    zcols = zcols[:, 0]
    gcols = gcols[:, 0]
    core = jnp.einsum("arp,bsp->arbs", yrows, gcols, precision=highest)
    left = jnp.einsum("arp,arbs->apbs", xrows, core, precision=highest)
    change = jnp.einsum("apbs,bsq->apbq", left, zcols, precision=highest)
    trail_out = trail - change[:, None, :, :, None, :]
    pcore = jnp.einsum("arp,sp->ars", yrows, pivot_scaled, precision=highest)
    pleft = jnp.einsum("arp,ars->aps", xrows, pcore, precision=highest)
    updated = panel[:, 0] - jnp.einsum("aps,sq->apq", pleft, pivot_basis, precision=highest)
    scaled_t = pair_apply(sketch, pair_kind, pivot_values)
    column_ids = lax.axis_index("col") * block + jnp.arange(block, dtype=jnp.int32)
    selector = (perm[:, None] == column_ids[None, :]).astype(jnp.float32)
    local_sketch = jnp.dot(scaled_t, selector, precision=highest)
    partial_range = jnp.einsum("apq,rq->arp", updated, local_sketch, precision=highest)
    range_t = total_of_pieces(partial_range, "col")
    gram = jnp.einsum("arp,asp->ars", range_t, range_t, precision=highest) / width
    basis = tri_solve(jnp.linalg.cholesky(gram), range_t)
    projected_part = jnp.einsum("arp,apq->arq", basis, updated, precision=highest)
    projected = lax.all_gather(projected_part, "col", axis=2, tiled=True)
    permuted = jnp.take(projected, perm, axis=2)
    coeff = pair_apply(permuted, pair_kind, pivot_values) / jnp.sqrt(jnp.float32(width))
    return (trail_out, basis[:, None], coeff[:, None])


def solution(mesh):
    return jax.shard_map(
        body,
        mesh=mesh,
        in_specs=(
            P(None, "row", None, None, "col", None),
            P(None, "row", None, "col"),
            P(None, "row", None, "col"),
            P(None, "row", None, "col"),
            P(None, "col", None, "row"),
            P(None, "col", None, "row"),
            P(None, "col"),
            P(),
            P(),
            P(),
            P(),
            P(),
        ),
        out_specs=(
            P(None, "row", None, None, "col", None),
            P(None, "row", None, None),
            P(None, "row", None, None),
        ),
        check_vma=False,
    )
```

profile of v0, /device:TPU:1, one launch (start us, length us, event | category | flops | bytes accessed | tf_op | source)
XLA Modules:
  0.0 150.3 jit_solution(10058551639044590301)
XLA Ops:
  7.2 0.0 copy-start
  7.2 0.0 copy-start.5
  7.2 0.0 copy-start.6
  7.2 0.0 copy-start.2
  7.2 0.0 copy-start.3
  7.2 0.0 copy-start.4
  7.2 0.0 all-gather.3.cloned.1.call-start
  7.3 0.8 broadcast_compare_fusion
  8.0 0.8 fusion.11
  8.8 0.8 copy.78
  9.6 0.1 reshape.159
  9.7 0.8 copy.79
  10.5 0.1 reshape.160
  10.6 1.0 copy.85
  11.6 22.7 %all_gather.16 = f32[512,256]{1,0:T(8,128)S(1)} all-gather(f32[32,256]{1,0:T(8,128)S(1)} %pad_maximum_fusion.2), channel_id=1, replica_groups=mesh['row'=16,'col'=16] {'col'}, dimensions={0}, use_global_device_ids=true | all-gather | bytes 557056 | tf_op jit(solution)/shard_map/all_gather | solution.py:10
  34.4 0.1 copy.81
  34.6 0.1 copy.80
  34.7 2.2 %broadcast_select_fusion.3 = (f32[64,256,1]{0,2,1:T(1,128)S(1)}, f32[64,256,1]{0,2,1:T(1,128)S(1)}) fusion(pred[256]{0:T(512)(128)(4,1)S(1)} %broadcast_compare_fusion, f32[64,256,2]{0,2,1:T(2,128)S(1)} %bitcast.108, f32[256]{0:T(256)S(1)} %bitcast.120, f32[256]{0:T(256)S(1)} %bitcast.126, f32[256]{0:T(256)S(1)} %bitcast.123, f32[256]{0:T(256)S(1)} %bitcast.117), kind=kLoop, calls=%fused_computation.11 | loop fusion | flops 196608 | bytes 266496 | tf_op jit(solution)/shard_map/jit(_where)/select_n | solution.py:31
  36.9 0.3 pad_maximum_fusion
  37.2 0.0 copy-done
  37.2 0.5 fusion.1
  37.7 0.4 fusion.14
  38.1 0.0 copy-done.5
  38.1 0.4 convolution_bitcast_fusion.1
  38.5 0.0 copy-done.6
  38.5 0.0 copy-done.2
  38.5 0.3 convolution_subtract_fusion
  38.8 1.1 convolution_bitcast_fusion
  40.0 0.0 all-gather.3.cloned.1.call-update
  40.0 0.2 broadcast_in_dim.45
  40.2 0.0 copy-done.3
  40.2 0.1 reshape.156
  40.3 0.0 copy-done.4
  40.3 0.1 reshape.157
  40.4 19.9 %all_gather.15 = f32[512,256]{1,0:T(8,128)S(1)} all-gather(f32[32,256]{1,0:T(8,128)S(1)} %pad_maximum_fusion.1), channel_id=1, replica_groups=mesh['row'=16,'col'=16] {'row'}, dimensions={0}, use_global_device_ids=true | all-gather | bytes 557056 | tf_op jit(solution)/shard_map/all_gather | solution.py:10
  60.3 0.1 copy.82
  60.5 0.1 copy.77
  60.6 11.0 %copy.84 = f32[2,1,512,2,1,512]{2,5,0,3,4,1:T(8,128)} copy(f32[2,1,512,2,1,512]{5,4,3,2,1,0:T(1,128)} %param.12) | data formatting | bytes 8388608 | tf_op args[0]
  71.6 0.5 fusion.12
  72.1 0.6 fusion.13
  72.7 6.7 %bitcast_subtract_fusion = f32[2,1,512,2,1,512]{2,5,0,3,4,1:T(8,128)} fusion(f32[2,1,512,2,1,512]{2,5,0,3,4,1:T(8,128)} %copy.84, f32[2,64,512,1]{2,1,3,0:T(8,128)S(1)} %bitcast.109, f32[2,512,2,64]{1,3,0,2:T(8,128)S(1)} %fusion.13), kind=kOutput, calls=%fused_computation.1 | convolution fusion | flops 806354944 | bytes 9175040 | tf_op jit(solution)/shard_map/apbs,bsq->apbq/dot_general | solution.py:71
  79.4 10.9 %copy.91 = f32[2,1,512,2,1,512]{5,4,3,2,1,0:T(1,128)} copy(f32[2,1,512,2,1,512]{2,5,0,3,4,1:T(8,128)} %bitcast_subtract_fusion) | data formatting | bytes 8388608
  90.3 0.0 all-gather.3.cloned.1.call-done
  90.3 2.6 %reduce_sum.9 = f32[2,64,512]{2,1,0:T(8,128)S(1)} reduce(f32[16,2,64,512]{3,2,1,0:T(8,128)} %bitcast.101, f32[]{:T(128)} %constant.67.clone.1), dimensions={0}, to_apply=%region_0.1 | reduce | flops 983040 | bytes 4456452 | tf_op jit(solution)/shard_map/reduce_sum | solution.py:19
  93.0 0.4 fusion.15
  93.4 0.1 copy.87
  93.5 11.7 %custom-call.8 = f32[2,64,64]{2,1,0:T(8,128)S(1)} custom-call(f32[2,64,64]{2,1,0:T(8,128)S(1)} %fusion.7), custom_call_target="Cholesky" | custom-call | tf_op jit(solution)/shard_map/jit(cholesky)/cholesky | solution.py:83
  105.2 0.1 compare_reduce_fusion
  105.3 0.1 select_bitcast_fusion
  105.4 9.8 %custom-call.9 = f32[2,1,64,64]{2,3,1,0:T(8,128)S(1)} custom-call(f32[2,1,64,64]{3,2,1,0:T(8,128)S(1)} %select_bitcast_fusion), custom_call_target="InvertDiagBlocksLowerTriangular" | custom-call | tf_op jit(solution)/shard_map/vmap(jit(_solve_triangular))/triangular_solve | solution.py:41
  115.3 0.4 fusion.5
  115.7 0.0 copy-start.1
  115.7 0.3 fusion.16
  116.1 20.6 %all_gather.19 = f32[2,64,512]{1,2,0:T(8,128)S(1)} all-gather(f32[2,64,32]{1,2,0:T(8,128)S(1)} %fusion.16), channel_id=1, replica_groups=mesh['row'=16,'col'=16] {'col'}, dimensions={2}, use_global_device_ids=true | all-gather | bytes 278528 | tf_op jit(solution)/shard_map/all_gather | solution.py:85
  136.6 0.4 copy.89
  137.0 2.1 %gather_fusion = f32[512,2,64]{2,1,0:T(2,128)S(1)} fusion(f32[2,64,512]{1,0,2:T(2,128)S(1)} %copy.89, s32[1024]{0:T(1024)S(1)} %pad_clamp_fusion), kind=kCustom, calls=%fused_computation | custom fusion | bytes 526336 | tf_op jit(solution)/shard_map/jit(_take)/gather | solution.py:86
  139.1 0.6 copy_select_fusion
  139.8 2.2 %broadcast_select_fusion.1 = (f32[2,64,256,1]{1,3,2,0:T(1,128)S(1)}, f32[2,64,256,1]{1,3,2,0:T(1,128)S(1)}) fusion(pred[256]{0:T(512)(128)(4,1)S(1)} %broadcast_compare_fusion, f32[2,64,256,2]{1,3,2,0:T(2,128)S(1)} %copy_select_fusion, f32[256]{0:T(256)S(1)} %bitcast.122, f32[256]{0:T(256)S(1)} %multiply_subtract_fusion, f32[256]{0:T(256)S(1)} %bitcast.125, ...), kind=kLoop, calls=%fused_computation.8 | loop fusion | flops 393216 | bytes 528640 | tf_op jit(solution)/shard_map/jit(_where)/select_n | solution.py:31
  142.0 0.6 maximum_multiply_fusion
  142.6 0.9 copy.93
  143.5 0.0 copy-done.1
  (15 shorter events, 0.2 us)
Async XLA Ops:
  7.2 30.0 %copy-start = (f32[64,512]{1,0:T(8,128)S(1)}, f32[64,512]{1,0:T(8,128)}, u32[]{:S(2)}) copy-start(f32[64,512]{1,0:T(8,128)} %param.19) | copy-start | bytes 393220
  7.2 30.9 %copy-start.5 = (s32[512]{0:T(512)S(1)}, s32[512]{0:T(512)}, u32[]{:S(2)}) copy-start(s32[512]{0:T(512)} %param.21) | copy-start | bytes 6148
  7.2 31.3 %copy-start.6 = (f32[64,32]{0,1:T(8,128)S(1)}, f32[64,32]{0,1:T(8,128)}, u32[]{:S(2)}) copy-start(f32[64,32]{0,1:T(8,128)} %param.18) | copy-start | bytes 24580
  7.2 31.3 %copy-start.2 = (f32[2,1,512,32]{2,3,1,0:T(8,128)S(1)}, f32[2,1,512,32]{2,3,1,0:T(8,128)}, u32[]{:S(2)}) copy-start(f32[2,1,512,32]{2,3,1,0:T(8,128)} %param.13) | copy-start | bytes 393220
  7.2 33.0 %copy-start.3 = (f32[2,1,64,32]{2,3,1,0:T(8,128)S(1)}, f32[2,1,64,32]{2,3,1,0:T(8,128)}, u32[]{:S(2)}) copy-start(f32[2,1,64,32]{2,3,1,0:T(8,128)} %param.16) | copy-start | bytes 49156
  7.2 33.1 %copy-start.4 = (f32[2,1,64,32]{2,3,1,0:T(8,128)S(1)}, f32[2,1,64,32]{2,3,1,0:T(8,128)}, u32[]{:S(2)}) copy-start(f32[2,1,64,32]{2,3,1,0:T(8,128)} %param.17) | copy-start | bytes 49156
  7.2 83.1 %all-gather.3.cloned.1.call-start = ((), (), s32[]{:S(2)}) async-start(), calls=%async_computation | async-start | bytes 4456448 | tf_op jit(solution)/shard_map/all_gather | solution.py:19
  115.7 27.8 %copy-start.1 = (f32[2,64,512]{2,1,0:T(8,128)}, f32[2,64,512]{2,1,0:T(8,128)S(1)}, u32[]{:S(2)}) copy-start(f32[2,64,512]{2,1,0:T(8,128)S(1)} %fusion.5) | copy-start | bytes 786436
Sparse Core Ops, SparseCore 0:
  40.1 40.0 all-gather.2
where the time goes:
time: 151 us; the launch traced here: 150 us
  blocking collectives  63.2 us (42%)
  other arithmetic  32 us (21%)
  local copies, waits for them, and re-layouts  29.1 us (19%)
  between operations  14.4 us (10%)
  matrix products  11.7 us (8%)
    all_gather x2, blocking collectives, gather_turned(): filled, at, outs = (lax.all_gather(both, axis, axis=0, tiled=True), 0, [])  42.6 us
    unnamed x18, local copies, waits for them, and re-layouts  23.8 us
    all_gather x1, blocking collectives, body(): projected = lax.all_gather(projected_part, 'col', axis=2, tiled=True)  20.6 us
    another operation x4, other arithmetic, body(): basis = tri_solve(jnp.linalg.cholesky(gram), range_t)  11.9 us
    another operation x3, other arithmetic, tri_solve(): jax.scipy.linalg.solve_triangular(low, right, lower=True)  9.92 us
    dot_general x1, matrix products, body(): change = jnp.einsum('apbs,bsq->apbq', left, zcols, precision=highest)  6.7 us
    select_n x2, other arithmetic, pair_apply(): jnp.where(twin, (first_in * diag_two - second_in * offdiag) / determinant...  4.37 us
  transfers between devices with their start and end apart: 1, of which 0 were waited for; matrix products, arithmetic and copies ran while one was open for 20% of the time, Pallas kernels for 0%

commit v1 on v0

--- a/solution.py
+++ b/solution.py
@@ -7,7 +7,13 @@
 def gather_turned(arrays, axis, dims):
     turned = [jnp.moveaxis(a, dim, 0) for a, dim in zip(arrays, dims)]
     both = jnp.concatenate([t.reshape(len(t), -1) for t in turned], axis=1)
-    filled, at, outs = (lax.all_gather(both, axis, axis=0, tiled=True), 0, [])
+    filled, at, outs = (
+        jnp.concatenate(
+            lax.all_to_all(jnp.stack([both] * lax.axis_size(axis)), axis, 0, 0), axis=0
+        ),
+        0,
+        [],
+    )
     for t, dim in zip(turned, dims):
         share = filled[:, at : at + t[0].size].reshape(-1, *t.shape[1:])
         outs.append(jnp.moveaxis(share, 0, dim))

time: 151 us -> 137 us (0.907)
  blocking collectives: 63.2 us -> 17.8 us
  starting transfers between devices: 0.04 us -> 16.8 us
  waiting for transfers between devices: 0.04 us -> 12.3 us
  local copies, waits for them, and re-layouts: 29.1 us -> 30.9 us
    all_gather x2 -> x0, blocking collectives: 42.6 us -> none  [gather_turned(): filled, at, outs = (lax.all_gather(both, axis, axis=0, tiled=True), 0, [])]
    all_to_all x0 -> x2, starting transfers between devices: none -> 16.7 us  [gather_turned(): lax.all_to_all(jnp.stack([both] * lax.axis_size(axis)), axis, 0, 0)]
    all_to_all x0 -> x2, waiting for transfers between devices: none -> 11.2 us  [gather_turned(): lax.all_to_all(jnp.stack([both] * lax.axis_size(axis)), axis, 0, 0)]
    all_gather x1, blocking collectives: 20.6 us -> 17.8 us  [body(): projected = lax.all_gather(projected_part, 'col', axis=2, tiled=True)]
    another operation x0 -> x2, local copies, waits for them, and re-layouts: none -> 1.7 us  [gather_turned(): jnp.stack([both] * lax.axis_size(axis))]
  transfers between devices with their start and end apart: 1 -> 3, of which waited for: 0 -> 3; matrix products, arithmetic and copies ran while one was open for 20% -> 27% of each run, Pallas kernels for 0% -> 0%
where the time goes in v1:
time: 137 us; the launch traced here: 136 us
  other arithmetic  31.9 us (23%)
  local copies, waits for them, and re-layouts  30.9 us (23%)
  blocking collectives  17.8 us (13%)
  starting transfers between devices  16.8 us (12%)
  between operations  14.4 us (11%)
  matrix products  12.3 us (9%)
  waiting for transfers between devices  12.3 us (9%)
    unnamed x18, local copies, waits for them, and re-layouts  23.8 us
    all_gather x1, blocking collectives, body(): projected = lax.all_gather(projected_part, 'col', axis=2, tiled=True)  17.8 us
    all_to_all x2, starting transfers between devices, gather_turned(): lax.all_to_all(jnp.stack([both] * lax.axis_size(axis)), axis, 0, 0)  16.7 us
    another operation x4, other arithmetic, body(): basis = tri_solve(jnp.linalg.cholesky(gram), range_t)  11.9 us
    all_to_all x2, waiting for transfers between devices, gather_turned(): lax.all_to_all(jnp.stack([both] * lax.axis_size(axis)), axis, 0, 0)  11.2 us
    another operation x3, other arithmetic, tri_solve(): jax.scipy.linalg.solve_triangular(low, right, lower=True)  9.92 us
    dot_general x1, matrix products, body(): change = jnp.einsum('apbs,bsq->apbq', left, zcols, precision=highest)  6.69 us
    select_n x2, other arithmetic, pair_apply(): jnp.where(twin, (first_in * diag_two - second_in * offdiag) / determinant...  4.34 us
  transfers between devices with their start and end apart: 3, of which 3 were waited for; matrix products, arithmetic and copies ran while one was open for 27% of the time, Pallas kernels for 0%

profile of v1, /device:TPU:1, one launch (start us, length us, event | category | flops | bytes accessed | tf_op | source)
XLA Modules:
  0.0 136.3 jit_solution(15535889499877135781)
XLA Ops:
  7.2 0.0 copy-start
  7.2 0.0 copy-start.6
  7.2 0.0 copy-start.2
  7.2 0.0 copy-start.3
  7.2 0.0 copy-start.4
  7.2 0.9 copy.77
  8.1 0.1 reshape.170
  8.2 0.8 copy.78
  9.0 0.1 reshape.171
  9.1 0.8 stack.9
  9.9 10.0 %all-to-all-start.1 = ((f32[16,32,256]{2,1,0:T(8,128)}), f32[16,32,256]{2,1,0:T(8,128)S(1)}, u32[]{:S(2)}, u32[]{:S(2)}) async-start(f32[16,32,256]{2,1,0:T(8,128)} %stack.9), calls=%async_computation.1 | async-start | bytes 1048576 | tf_op jit(solution)/shard_map/all_to_all | solution.py:12
  19.9 0.0 all-gather.3.cloned.1.call-start
  19.9 0.8 fusion.11
  20.8 1.0 copy.84
  21.8 0.7 broadcast_compare_fusion
  22.5 2.1 %broadcast_select_fusion.3 = (f32[64,256,1]{0,2,1:T(1,128)S(1)}, f32[64,256,1]{0,2,1:T(1,128)S(1)}) fusion(pred[256]{0:T(512)(128)(4,1)S(1)} %broadcast_compare_fusion, f32[64,256,2]{0,2,1:T(2,128)S(1)} %bitcast.113, f32[256]{0:T(256)S(1)} %bitcast.124, f32[256]{0:T(256)S(1)} %bitcast.130, f32[256]{0:T(256)S(1)} %bitcast.127, f32[256]{0:T(256)S(1)} %bitcast.121), kind=kLoop, calls=%fused_computation.11 | loop fusion | flops 196608 | bytes 266496 | tf_op jit(solution)/shard_map/jit(_where)/select_n | solution.py:37
  24.6 0.3 pad_maximum_fusion
  24.9 1.1 convolution_bitcast_fusion.1
  26.1 11.0 %all-to-all-done.1 = f32[16,32,256]{2,1,0:T(8,128)S(1)} async-done(((f32[16,32,256]{2,1,0:T(8,128)}), f32[16,32,256]{2,1,0:T(8,128)S(1)}, u32[]{:S(2)}, u32[]{:S(2)}) %all-to-all-start.1) | async-done | bytes 524320 | tf_op jit(solution)/shard_map/all_to_all | solution.py:12
  37.1 0.1 copy.80
  37.3 0.1 copy.79
  37.4 0.0 copy-done
  37.4 0.5 fusion.1
  37.9 0.4 fusion.14
  38.3 0.0 copy-done.6
  38.3 0.0 copy-done.2
  38.3 0.3 convolution_subtract_fusion
  38.6 1.1 convolution_bitcast_fusion
  39.7 0.0 all-gather.3.cloned.1.call-update
  39.7 0.0 copy-done.3
  39.8 0.1 reshape.166
  39.9 0.0 copy-done.4
  39.9 0.1 reshape.167
  40.0 0.9 stack.8
  40.9 6.8 %all-to-all-start = ((f32[16,32,256]{2,1,0:T(8,128)}), f32[16,32,256]{2,1,0:T(8,128)S(1)}, u32[]{:S(2)}, u32[]{:S(2)}) async-start(f32[16,32,256]{2,1,0:T(8,128)} %stack.8), calls=%async_computation | async-start | bytes 1048576 | tf_op jit(solution)/shard_map/all_to_all | solution.py:12
  47.6 0.0 copy-done.5
  47.7 0.2 broadcast_in_dim.45
  47.9 10.9 %copy.83 = f32[2,1,512,2,1,512]{2,5,0,3,4,1:T(8,128)} copy(f32[2,1,512,2,1,512]{5,4,3,2,1,0:T(1,128)} %param.12) | data formatting | bytes 8388608 | tf_op args[0]
  58.8 0.2 all-to-all-done
  59.0 0.1 copy.81
  59.2 0.1 copy.76
  59.3 0.5 fusion.12
  59.8 0.6 fusion.13
  60.4 6.7 %bitcast_subtract_fusion = f32[2,1,512,2,1,512]{2,5,0,3,4,1:T(8,128)} fusion(f32[2,1,512,2,1,512]{2,5,0,3,4,1:T(8,128)} %copy.83, f32[2,64,512,1]{2,1,3,0:T(8,128)S(1)} %bitcast.112, f32[2,512,2,64]{1,3,0,2:T(8,128)S(1)} %fusion.13), kind=kOutput, calls=%fused_computation.1 | convolution fusion | flops 806354944 | bytes 9175040 | tf_op jit(solution)/shard_map/apbs,bsq->apbq/dot_general | solution.py:77
  67.1 10.9 %copy.90 = f32[2,1,512,2,1,512]{5,4,3,2,1,0:T(1,128)} copy(f32[2,1,512,2,1,512]{2,5,0,3,4,1:T(8,128)} %bitcast_subtract_fusion) | data formatting | bytes 8388608
  78.0 1.0 all-gather.3.cloned.1.call-done
  79.1 2.6 %reduce_sum.9 = f32[2,64,512]{2,1,0:T(8,128)S(1)} reduce(f32[16,2,64,512]{3,2,1,0:T(8,128)} %bitcast.103, f32[]{:T(128)} %constant.67.clone.1), dimensions={0}, to_apply=%region_0.1 | reduce | flops 983040 | bytes 4456452 | tf_op jit(solution)/shard_map/reduce_sum | solution.py:25
  81.7 0.4 fusion.15
  82.1 0.1 copy.86
  82.2 11.7 %custom-call.8 = f32[2,64,64]{2,1,0:T(8,128)S(1)} custom-call(f32[2,64,64]{2,1,0:T(8,128)S(1)} %fusion.7), custom_call_target="Cholesky" | custom-call | tf_op jit(solution)/shard_map/jit(cholesky)/cholesky | solution.py:89
  94.0 0.1 compare_reduce_fusion
  94.1 0.1 select_bitcast_fusion
  94.2 9.8 %custom-call.9 = f32[2,1,64,64]{2,3,1,0:T(8,128)S(1)} custom-call(f32[2,1,64,64]{3,2,1,0:T(8,128)S(1)} %select_bitcast_fusion), custom_call_target="InvertDiagBlocksLowerTriangular" | custom-call | tf_op jit(solution)/shard_map/vmap(jit(_solve_triangular))/triangular_solve | solution.py:47
  104.0 0.4 fusion.5
  104.4 0.0 copy-start.1
  104.5 0.3 fusion.16
  104.8 17.8 %all_gather.11 = f32[2,64,512]{1,2,0:T(8,128)S(1)} all-gather(f32[2,64,32]{1,2,0:T(8,128)S(1)} %fusion.16), channel_id=1, replica_groups=mesh['row'=16,'col'=16] {'col'}, dimensions={2}, use_global_device_ids=true | all-gather | bytes 278528 | tf_op jit(solution)/shard_map/all_gather | solution.py:91
  122.6 0.4 copy.88
  123.0 2.1 %gather_fusion = f32[512,2,64]{2,1,0:T(2,128)S(1)} fusion(f32[2,64,512]{1,0,2:T(2,128)S(1)} %copy.88, s32[1024]{0:T(1024)S(1)} %pad_clamp_fusion), kind=kCustom, calls=%fused_computation | custom fusion | bytes 526336 | tf_op jit(solution)/shard_map/jit(_take)/gather | solution.py:92
  125.1 0.6 copy_select_fusion
  125.7 2.2 %broadcast_select_fusion.1 = (f32[2,64,256,1]{1,3,2,0:T(1,128)S(1)}, f32[2,64,256,1]{1,3,2,0:T(1,128)S(1)}) fusion(pred[256]{0:T(512)(128)(4,1)S(1)} %broadcast_compare_fusion, f32[2,64,256,2]{1,3,2,0:T(2,128)S(1)} %copy_select_fusion, f32[256]{0:T(256)S(1)} %bitcast.126, f32[256]{0:T(256)S(1)} %multiply_subtract_fusion, f32[256]{0:T(256)S(1)} %bitcast.129, ...), kind=kLoop, calls=%fused_computation.8 | loop fusion | flops 393216 | bytes 528640 | tf_op jit(solution)/shard_map/jit(_where)/select_n | solution.py:37
  127.9 0.6 maximum_multiply_fusion
  128.6 0.9 copy.92
  129.4 0.0 copy-done.1
  (16 shorter events, 0.2 us)
Async XLA Ops:
  7.2 30.2 %copy-start = (f32[64,512]{1,0:T(8,128)S(1)}, f32[64,512]{1,0:T(8,128)}, u32[]{:S(2)}) copy-start(f32[64,512]{1,0:T(8,128)} %param.19) | copy-start | bytes 393220
  7.2 31.1 %copy-start.6 = (f32[64,32]{0,1:T(8,128)S(1)}, f32[64,32]{0,1:T(8,128)}, u32[]{:S(2)}) copy-start(f32[64,32]{0,1:T(8,128)} %param.18) | copy-start | bytes 24580
  7.2 31.1 %copy-start.2 = (f32[2,1,512,32]{2,3,1,0:T(8,128)S(1)}, f32[2,1,512,32]{2,3,1,0:T(8,128)}, u32[]{:S(2)}) copy-start(f32[2,1,512,32]{2,3,1,0:T(8,128)} %param.13) | copy-start | bytes 393220
  7.2 32.5 %copy-start.3 = (f32[2,1,64,32]{2,3,1,0:T(8,128)S(1)}, f32[2,1,64,32]{2,3,1,0:T(8,128)}, u32[]{:S(2)}) copy-start(f32[2,1,64,32]{2,3,1,0:T(8,128)} %param.16) | copy-start | bytes 49156
  7.2 32.7 %copy-start.4 = (f32[2,1,64,32]{2,3,1,0:T(8,128)S(1)}, f32[2,1,64,32]{2,3,1,0:T(8,128)}, u32[]{:S(2)}) copy-start(f32[2,1,64,32]{2,3,1,0:T(8,128)} %param.17) | copy-start | bytes 49156
  9.9 27.2 %all-to-all-start.1 = ((f32[16,32,256]{2,1,0:T(8,128)}), f32[16,32,256]{2,1,0:T(8,128)S(1)}, u32[]{:S(2)}, u32[]{:S(2)}) async-start(f32[16,32,256]{2,1,0:T(8,128)} %stack.9), calls=%async_computation.1 | async-start | bytes 1048576 | tf_op jit(solution)/shard_map/all_to_all | solution.py:12
  19.9 27.8 %copy-start.5 = (s32[512]{0:T(512)S(1)}, s32[512]{0:T(512)}, u32[]{:S(2)}) copy-start(s32[512]{0:T(512)} %param.21) | copy-start | bytes 6148
  19.9 59.2 %all-gather.3.cloned.1.call-start = ((), (), s32[]{:S(2)}) async-start(), calls=%async_computation.2 | async-start | bytes 4456448 | tf_op jit(solution)/shard_map/all_gather | solution.py:25
  40.9 18.1 %all-to-all-start = ((f32[16,32,256]{2,1,0:T(8,128)}), f32[16,32,256]{2,1,0:T(8,128)S(1)}, u32[]{:S(2)}, u32[]{:S(2)}) async-start(f32[16,32,256]{2,1,0:T(8,128)} %stack.8), calls=%async_computation | async-start | bytes 1048576 | tf_op jit(solution)/shard_map/all_to_all | solution.py:12
  104.4 25.0 %copy-start.1 = (f32[2,64,512]{2,1,0:T(8,128)}, f32[2,64,512]{2,1,0:T(8,128)S(1)}, u32[]{:S(2)}) copy-start(f32[2,64,512]{2,1,0:T(8,128)S(1)} %fusion.5) | copy-start | bytes 786436
Sparse Core Ops, SparseCore 0:
  39.9 39.1 all-gather.2
